TPU v7x, 128 devices: a whole 4x4x4 slice. The times are simulated.
128 devices in a mesh: blk: 8 (over x, z_hi), grp: 16 (over z_lo, y, core).
Axes of the slice: x: 4, y: 4, z: 4 (z_hi: 2, z_lo: 2; z = z_hi * 2 + z_lo), core: 2. Of those that a mesh axis runs over, the one named last changes fastest.
Arguments:
- frames: bfloat16 [16384, 8, 2048], P(('blk', 'grp')), may hold values from -6 to 6
- counts: int32 [16384], P(('blk', 'grp')), may hold values from 1 to 8
- positives: int32 [16384], P(('blk', 'grp')), may hold values from 0 to 16383, as said below
- w_first: bfloat16 [2048, 4096], P(None, 'grp'), may hold values from -0.125 to 0.125
- w_second: bfloat16 [4096, 256], P('grp'), may hold values from -0.09375 to 0.09375
Outputs:
- batch_loss: float32 [], replicated
- grad_first: float32 [2048, 4096], P(None, 'grp')
- grad_second: float32 [4096, 256], P('grp')
Inputs may be any that keep to these rules, and one draw needn't show every extreme that they name: positives[positives[i]] = i and positives[i] != i for every clip i.
All inputs are finite; a program needn't handle non-finite values.
Results may differ from a plain program's by a relative error of at most 0.005.
The roundings to bfloat16 on the way count: a program that leaves them out, or rounds other values in their place, can miss the bound.
Values may be sent and summed in bfloat16 or wider, within the bound.
No kernel may reach another device: no remote copies, remote signals or barrier semaphores. Data moves between devices by JAX's collectives and lax.ppermute only.
A program may use at most 128 MiB of HBM per device.

v0:
```python
import jax
import jax.numpy as jnp
from jax import lax
from jax.sharding import Mesh
from jax.sharding import PartitionSpec as P

BLK = ("blk_0", "blk_1")
GRP = ("grp_0", "grp_1", "grp_2")
BLK_GRP = ("blk_0", "blk_1", "grp_0", "grp_1", "grp_2")
logit_sharpness_divisor = 0.05
score_top = 20.0


def in_blocks(array, dim, peers):
    shape = array.shape
    pieces = array.reshape(*shape[:dim], peers, shape[dim] // peers, *shape[dim + 1 :])
    return jnp.moveaxis(pieces, dim, 0)


def sent_and_summed(array, axis, dim):
    peers = lax.axis_size(axis)
    pieces = lax.all_to_all(in_blocks(array, dim, peers), axis, 0, 0, tiled=True)
    return jnp.sum(pieces, axis=0)


def in_order(pieces, dim):
    shape = list(pieces.shape[1:])
    shape[dim] *= pieces.shape[0]
    return jnp.moveaxis(pieces, 0, dim).reshape(shape)


def from_everyone(array, axis):
    peers = lax.axis_size(axis)
    return lax.all_to_all(
        jnp.broadcast_to(array[None], (peers, *array.shape)), axis, 0, 0, tiled=True
    )


def gather_directly(array, axis, dim):
    return in_order(from_everyone(array, axis), dim)


def shifted(block, axis, distance):
    devices = range(lax.axis_size(axis))
    route = [((i - distance) % len(devices), i) for i in devices]
    return lax.ppermute(block, axis, route)


def by_axis(array, axes):
    for axis in axes:
        array = lax.psum(array, axis)
    return array


def shards(frames, counts, positives, w_first, w_second):
    row_count = frames.shape[0]
    slot_count = frames.shape[1]
    cycle_size = lax.axis_size(BLK)
    group_size = lax.axis_size(GRP)
    complete_segment_entries = row_count * cycle_size * group_size
    group_rows = row_count * group_size
    cycle_index = lax.axis_index(BLK)
    first_row = (cycle_index * group_size + lax.axis_index(GRP)) * row_count
    row_ids = first_row + jnp.arange(row_count, dtype=jnp.int32)
    frame_mask = (jnp.arange(slot_count, dtype=jnp.int32)[None, :] < counts[:, None]).astype(
        jnp.bfloat16
    )
    summed = jnp.einsum("rf,rfc->rc", frame_mask, frames, preferred_element_type=jnp.float32)
    pooled = (summed / counts[:, None].astype(jnp.float32)).astype(jnp.bfloat16)
    pooled_all = lax.all_gather(pooled, GRP, axis=0, tiled=True)
    preact = jnp.dot(pooled_all, w_first, preferred_element_type=jnp.float32)
    hidden = jax.nn.gelu(preact).astype(jnp.bfloat16)
    raw_keys = sent_and_summed(
        jnp.dot(hidden, w_second, preferred_element_type=jnp.float32), GRP, 0
    )
    key_length = jnp.sqrt(jnp.sum(raw_keys * raw_keys, axis=1, keepdims=True) + 1e-06)
    unit_keys = raw_keys / key_length
    lower_match_vectors = unit_keys.astype(jnp.bfloat16)
    key_block = gather_directly(lower_match_vectors, GRP, 0)
    block_ids = jnp.arange(group_rows, dtype=jnp.int32)
    exp_total = jnp.zeros((row_count,), jnp.float32)
    pos_score = jnp.zeros((row_count,), jnp.float32)
    stored = []
    for hop_index in range(cycle_size):
        owner = (cycle_index - hop_index) % cycle_size
        offset = owner * group_rows
        key_ids = offset + block_ids
        cosine_logit_matrix = (
            lax.dot_general(
                lower_match_vectors,
                key_block,
                (((1,), (1,)), ((), ())),
                preferred_element_type=jnp.float32,
            )
            / logit_sharpness_divisor
        )
        self_mask = key_ids[None, :] == row_ids[:, None]
        pair_mask = key_ids[None, :] == positives[:, None]
        exp_total = exp_total + jnp.sum(
            jnp.where(self_mask, 0.0, jnp.exp(cosine_logit_matrix - score_top)), axis=1
        )
        pos_score = pos_score + jnp.sum(jnp.where(pair_mask, cosine_logit_matrix, 0.0), axis=1)
        stored.append((key_block, offset, cosine_logit_matrix, self_mask, pair_mask))
        if hop_index + 1 < cycle_size:
            key_block = shifted(key_block, BLK, 1)
    log_norm = jnp.log(exp_total) + score_top
    batch_loss = by_axis(jnp.sum(log_norm - pos_score), BLK_GRP) / complete_segment_entries
    query_gradient = jnp.zeros((row_count, lower_match_vectors.shape[1]), jnp.float32)
    every_norm = lax.all_gather(log_norm, BLK_GRP, axis=0, tiled=True)
    self_key_gradient = jnp.zeros((row_count, lower_match_vectors.shape[1]), jnp.float32)
    for key_block, offset, cosine_logit_matrix, self_mask, pair_mask in stored:
        pair_float = pair_mask.astype(jnp.float32)
        probs = jnp.where(self_mask, 0.0, jnp.exp(cosine_logit_matrix - log_norm[:, None]))
        weights = (probs - pair_float).astype(jnp.bfloat16)
        column_norm = lax.dynamic_slice_in_dim(every_norm, offset, group_rows, 0)
        mirrored = jnp.where(self_mask, 0.0, jnp.exp(cosine_logit_matrix - column_norm[None, :]))
        mirror_weights = (mirrored - pair_float).astype(jnp.bfloat16)
        query_gradient = query_gradient + jnp.dot(
            weights, key_block, preferred_element_type=jnp.float32
        )
        self_key_gradient = self_key_gradient + jnp.dot(
            mirror_weights, key_block, preferred_element_type=jnp.float32
        )
    sphere_projected_derivative = (query_gradient + self_key_gradient) / (
        complete_segment_entries * logit_sharpness_divisor
    )
    raw_grad = (
        (
            sphere_projected_derivative
            - unit_keys * jnp.sum(unit_keys * sphere_projected_derivative, axis=1, keepdims=True)
        )
        / key_length
    ).astype(jnp.bfloat16)
    group_grad = gather_directly(raw_grad, GRP, 0)
    second_grad = lax.dot_general(
        hidden, group_grad, (((0,), (0,)), ((), ())), preferred_element_type=jnp.float32
    )
    hidden_grad = lax.dot_general(
        group_grad, w_second, (((1,), (1,)), ((), ())), preferred_element_type=jnp.float32
    )
    unused, backward = jax.vjp(jax.nn.gelu, preact)
    preact_grad = backward(hidden_grad)[0].astype(jnp.bfloat16)
    first_grad = lax.dot_general(
        pooled_all, preact_grad, (((0,), (0,)), ((), ())), preferred_element_type=jnp.float32
    )
    first_grad, second_grad = lax.psum((first_grad, second_grad), BLK)
    return (batch_loss, first_grad, second_grad)


def solution(mesh):
    finer = Mesh(mesh.devices.reshape(4, 2, 2, 4, 2), ("blk_0", "blk_1", "grp_0", "grp_1", "grp_2"))
    placed = (P(BLK_GRP, None, None), P(BLK_GRP), P(BLK_GRP), P(None, GRP), P(GRP, None))
    return jax.shard_map(
        shards,
        mesh=finer,
        in_specs=placed,
        out_specs=(P(), P(None, GRP), P(GRP, None)),
        check_vma=False,
    )
```

profile of v0, /device:TPU:6, one launch (start us, length us, event | category | flops | bytes accessed | tf_op | source)
XLA Modules:
  0.0 521.7 jit_solution(11916011583549820062)
XLA Ops:
  8.7 3.4 fusion.148
  13.4 54.5 %all-gather.3.cloned.1.call-done = bf16[2048,2048]{1,0:T(8,128)(2,1)} async-done(((bf16[128,2048]{1,0:T(8,128)(2,1)}), bf16[2048,2048]{1,0:T(8,128)(2,1)}) %all-gather.3.cloned.1.call-update) | async-done | bytes 8388624 | tf_op jit(solution)/shard_map/all_gather | solution.py:70
  67.9 5.9 %fusion.179 = f32[2048,256]{1,0:T(8,128)S(1)} fusion(bf16[2048,2048]{1,0:T(8,128)(2,1)} %all-gather.3.cloned.1.call-done, bf16[2048,256]{1,0:T(8,128)(2,1)S(1)} %copy-done), kind=kOutput, calls=%fused_computation.252 | convolution fusion | flops 2147483648 | bytes 11534336 | tf_op jit(solution)/shard_map/dot_general | solution.py:71
  75.1 32.5 %all_to_all.15 = f32[16,128,256]{2,1,0:T(8,128)S(1)} all-to-all(f32[16,128,256]{2,1,0:T(8,128)S(1)} %bitcast.55), channel_id=1, replica_groups=mesh['blk_0'=4,'blk_1'=2,'grp_0'=2,'grp_1'=4,'grp_2'=2] {'grp_0','grp_1'..., dimensions={0} | all-to-all | bytes 4194304 | tf_op jit(solution)/shard_map/all_to_all | solution.py:22
  108.0 19.1 %all_to_all.16 = bf16[16,128,256]{2,1,0:T(8,128)(2,1)S(1)} all-to-all(bf16[16,128,256]{2,1,0:T(8,128)(2,1)S(1)} %broadcast_in_dim.41), channel_id=1, replica_groups=mesh['blk_0'=4,'blk_1'=2,'grp_0'=2,'grp_1'=4,'grp_2'=2] {'grp_0','grp_1'..., dimensions={0} | all-to-all | bytes 2097152 | tf_op jit(solution)/shard_map/all_to_all | solution.py:34
  129.9 23.7 %collective-permute-done = bf16[2048,256]{1,0:T(8,128)(2,1)S(1)} collective-permute-done((bf16[2048,256]{1,0:T(8,128)(2,1)S(1)}, bf16[2048,256]{1,0:T(8,128)(2,1)S(1)}, u32[]{:S(2)}, u32[]{:S(2)}) %collective-permute-start) | collective-permute-done | bytes 1048608 | tf_op jit(solution)/shard_map/ppermute | solution.py:46
  155.6 23.7 %collective-permute-done.1 = bf16[2048,256]{1,0:T(8,128)(2,1)S(1)} collective-permute-done((bf16[2048,256]{1,0:T(8,128)(2,1)S(1)}, bf16[2048,256]{1,0:T(8,128)(2,1)S(1)}, u32[]{:S(2)}, u32[]{:S(2)}) %collective-permute-start.1) | collective-permute-done | bytes 1048608 | tf_op jit(solution)/shard_map/ppermute | solution.py:46
  181.5 23.8 %collective-permute-done.2 = bf16[2048,256]{1,0:T(8,128)(2,1)S(1)} collective-permute-done((bf16[2048,256]{1,0:T(8,128)(2,1)S(1)}, bf16[2048,256]{1,0:T(8,128)(2,1)S(1)}, u32[]{:S(2)}, u32[]{:S(2)}) %collective-permute-start.2) | collective-permute-done | bytes 1048608 | tf_op jit(solution)/shard_map/ppermute | solution.py:46
  207.3 23.0 %collective-permute-done.3 = bf16[2048,256]{1,0:T(8,128)(2,1)} collective-permute-done((bf16[2048,256]{1,0:T(8,128)(2,1)S(1)}, bf16[2048,256]{1,0:T(8,128)(2,1)}, u32[]{:S(2)}, u32[]{:S(2)}) %collective-permute-start.3) | collective-permute-done | bytes 1048608 | tf_op jit(solution)/shard_map/ppermute | solution.py:46
  232.5 21.3 %collective-permute-done.4 = bf16[2048,256]{1,0:T(8,128)(2,1)} collective-permute-done((bf16[2048,256]{1,0:T(8,128)(2,1)}, bf16[2048,256]{1,0:T(8,128)(2,1)}, u32[]{:S(2)}, u32[]{:S(2)}) %collective-permute-start.4) | collective-permute-done | bytes 1048608 | tf_op jit(solution)/shard_map/ppermute | solution.py:46
  253.8 3.5 collective-permute-start.5
  259.0 18.3 %collective-permute-done.5 = bf16[2048,256]{1,0:T(8,128)(2,1)S(1)} collective-permute-done((bf16[2048,256]{1,0:T(8,128)(2,1)}, bf16[2048,256]{1,0:T(8,128)(2,1)S(1)}, u32[]{:S(2)}, u32[]{:S(2)}) %collective-permute-start.5) | collective-permute-done | bytes 1048608 | tf_op jit(solution)/shard_map/ppermute | solution.py:46
  277.3 3.7 collective-permute-start.6
  285.5 13.3 %collective-permute-done.6 = bf16[2048,256]{1,0:T(8,128)(2,1)S(1)} collective-permute-done((bf16[2048,256]{1,0:T(8,128)(2,1)S(1)}, bf16[2048,256]{1,0:T(8,128)(2,1)S(1)}, u32[]{:S(2)}, u32[]{:S(2)}) %collective-permute-start.6) | collective-permute-done | bytes 1048608 | tf_op jit(solution)/shard_map/ppermute | solution.py:46
  302.6 44.5 %all-gather = f32[128,1,128]{2,1,0:T(1,128)S(1)} all-gather(f32[1,1,128]{2,1,0:T(1,128)S(1)} %bitcast.59), channel_id=1, replica_groups=mesh['blk_0'=4,'blk_1'=2,'grp_0'=2,'grp_1'=4,'grp_2'=2] {'blk_0','blk_1'..., dimensions={0}, use_global_device_ids=true | all-gather | bytes 66048 | tf_op jit(solution)/shard_map/all_gather | solution.py:109
  359.7 20.1 %all_to_all.17 = bf16[16,128,256]{2,1,0:T(8,128)(2,1)S(1)} all-to-all(bf16[16,128,256]{2,1,0:T(8,128)(2,1)S(1)} %broadcast_in_dim.42), channel_id=1, replica_groups=mesh['blk_0'=4,'blk_1'=2,'grp_0'=2,'grp_1'=4,'grp_2'=2] {'grp_0','grp_1'..., dimensions={0} | all-to-all | bytes 2097152 | tf_op jit(solution)/shard_map/all_to_all | solution.py:34
  381.4 9.3 %fusion.41 = f32[2048,256]{1,0:T(8,128)} fusion(bf16[2048,2048]{1,0:T(8,128)(2,1)} %all-gather.3.cloned.1.call-done, f32[2048,256]{1,0:T(8,128)} %copy-done.8, bf16[2048,256]{1,0:T(8,128)(2,1)S(1)} %bitcast.57, bf16[256,256]{1,0:T(8,128)(2,1)S(1)} %copy-done.6), kind=kOutput, calls=%fused_computation.114 | convolution fusion | flops 2426404864 | bytes 13762560 | tf_op jit(solution)/shard_map/dot_general | solution.py:143
  390.7 8.9 %psum.49 = f32[]{:T(128)} all-reduce(f32[]{:T(128)} %get-tuple-element.35), channel_id=1, replica_groups=mesh['blk_0'=4,'blk_1'=2,'grp_0'=2,'grp_1'=4,'grp_2'=2] {'blk_0'}, use_global_device_ids=true, to_apply=%region_19.20 | all-reduce | flops 1 | bytes 8 | tf_op jit(solution)/shard_map/psum | solution.py:51
  399.6 7.3 %psum.50 = f32[]{:T(128)} all-reduce(f32[]{:T(128)} %psum.49), channel_id=1, replica_groups=mesh['blk_0'=4,'blk_1'=2,'grp_0'=2,'grp_1'=4,'grp_2'=2] {'blk_1'}, use_global_device_ids=true, to_apply=%region_20.21 | all-reduce | flops 1 | bytes 8 | tf_op jit(solution)/shard_map/psum | solution.py:51
  406.8 5.7 %psum.51 = f32[]{:T(128)} all-reduce(f32[]{:T(128)} %psum.50), channel_id=1, replica_groups=mesh['blk_0'=4,'blk_1'=2,'grp_0'=2,'grp_1'=4,'grp_2'=2] {'grp_0'}, use_global_device_ids=true, to_apply=%region_21.22 | all-reduce | flops 1 | bytes 8 | tf_op jit(solution)/shard_map/psum | solution.py:51
  412.6 10.6 %psum.52 = f32[]{:T(128)} all-reduce(f32[]{:T(128)} %psum.51), channel_id=1, replica_groups=mesh['blk_0'=4,'blk_1'=2,'grp_0'=2,'grp_1'=4,'grp_2'=2] {'grp_1'}, use_global_device_ids=true, to_apply=%region_22.23 | all-reduce | flops 1 | bytes 8 | tf_op jit(solution)/shard_map/psum | solution.py:51
  423.2 3.1 psum.53
  426.9 83.0 %all-reduce.3.cloned.1.call-done = (f32[2048,256]{1,0:T(8,128)}, f32[256,256]{1,0:T(8,128)}) async-done(((f32[2048,256]{1,0:T(8,128)}, f32[256,256]{1,0:T(8,128)}), (f32[2048,256]{1,0:T(8,128)}, f32[256,256]{1,0:T(8,128)})) %all-reduce.3.cloned.1.call-update) | async-done | bytes 2359312 | tf_op jit(solution)/shard_map/psum | solution.py:146
  509.9 3.1 copy.16
  (73 shorter events, 40.3 us)
Async XLA Ops:
  7.2 60.7 %copy-start = (bf16[2048,256]{1,0:T(8,128)(2,1)S(1)}, bf16[2048,256]{1,0:T(8,128)(2,1)}, u32[]{:S(2)}) copy-start(bf16[2048,256]{1,0:T(8,128)(2,1)} %param.8) | copy-start | bytes 3145732
  7.2 60.7 %all-gather.3.cloned.1.call-start = ((), (), s32[]{:S(2)}) async-start(), calls=%async_computation.3 | async-start | bytes 8912896 | tf_op jit(solution)/shard_map/all_gather | solution.py:70
  13.3 60.4 %copy-start.6 = (bf16[256,256]{1,0:T(8,128)(2,1)S(1)}, bf16[256,256]{1,0:T(8,128)(2,1)}, u32[]{:S(2)}) copy-start(bf16[256,256]{1,0:T(8,128)(2,1)} %param.9) | copy-start | bytes 393220
  13.3 496.6 %all-reduce.3.cloned.1.call-start = ((), (), s32[]{:S(2)}) async-start(), calls=%async_computation.4 | async-start | bytes 4718592 | tf_op jit(solution)/shard_map/psum | solution.py:146
  73.7 1.3 copy-start.8
  127.1 26.6 %collective-permute-start = (bf16[2048,256]{1,0:T(8,128)(2,1)S(1)}, bf16[2048,256]{1,0:T(8,128)(2,1)S(1)}, u32[]{:S(2)}, u32[]{:S(2)}) collective-permute-start(bf16[2048,256]{1,0:T(8,128)(2,1)S(1)} %bitcast.51), channel_id=1, source_target_pairs={{112,0},{0,16},{16,32},{32,48},{48,64},{64,80},{80,96},{96,112},{1... | collective-permute-start | bytes 3145736 | tf_op jit(solution)/shard_map/ppermute | solution.py:46
  153.7 25.7 %collective-permute-start.1 = (bf16[2048,256]{1,0:T(8,128)(2,1)S(1)}, bf16[2048,256]{1,0:T(8,128)(2,1)S(1)}, u32[]{:S(2)}, u32[]{:S(2)}) collective-permute-start(bf16[2048,256]{1,0:T(8,128)(2,1)S(1)} %collective-permute-done), channel_id=1, source_target_pairs={{112,0},{0,16},{16,32},{32,48},{48,64},{64,80},{80,96},{96,112},{1... | collective-permute-start | bytes 3145736 | tf_op jit(solution)/shard_map/ppermute | solution.py:46
  179.4 1.1 copy-start.1
  180.4 24.8 %collective-permute-start.2 = (bf16[2048,256]{1,0:T(8,128)(2,1)S(1)}, bf16[2048,256]{1,0:T(8,128)(2,1)S(1)}, u32[]{:S(2)}, u32[]{:S(2)}) collective-permute-start(bf16[2048,256]{1,0:T(8,128)(2,1)S(1)} %collective-permute-done.1), channel_id=1, source_target_pairs={{112,0},{0,16},{16,32},{32,48},{48,64},{64,80},{80,96},{96,112},{1... | collective-permute-start | bytes 3145736 | tf_op jit(solution)/shard_map/ppermute | solution.py:46
  205.3 1.0 copy-start.3
  206.2 24.1 %collective-permute-start.3 = (bf16[2048,256]{1,0:T(8,128)(2,1)S(1)}, bf16[2048,256]{1,0:T(8,128)(2,1)}, u32[]{:S(2)}, u32[]{:S(2)}) collective-permute-start(bf16[2048,256]{1,0:T(8,128)(2,1)S(1)} %collective-permute-done.2), channel_id=1, source_target_pairs={{112,0},{0,16},{16,32},{32,48},{48,64},{64,80},{80,96},{96,112},{1... | collective-permute-start | bytes 3145736 | tf_op jit(solution)/shard_map/ppermute | solution.py:46
  230.3 23.4 %collective-permute-start.4 = (bf16[2048,256]{1,0:T(8,128)(2,1)}, bf16[2048,256]{1,0:T(8,128)(2,1)}, u32[]{:S(2)}, u32[]{:S(2)}) collective-permute-start(bf16[2048,256]{1,0:T(8,128)(2,1)} %collective-permute-done.3), channel_id=1, source_target_pairs={{112,0},{0,16},{16,32},{32,48},{48,64},{64,80},{80,96},{96,112},{1... | collective-permute-start | bytes 3145736 | tf_op jit(solution)/shard_map/ppermute | solution.py:46
  253.8 23.5 %collective-permute-start.5 = (bf16[2048,256]{1,0:T(8,128)(2,1)}, bf16[2048,256]{1,0:T(8,128)(2,1)S(1)}, u32[]{:S(2)}, u32[]{:S(2)}) collective-permute-start(bf16[2048,256]{1,0:T(8,128)(2,1)} %collective-permute-done.4), channel_id=1, source_target_pairs={{112,0},{0,16},{16,32},{32,48},{48,64},{64,80},{80,96},{96,112},{1... | collective-permute-start | bytes 3145736 | tf_op jit(solution)/shard_map/ppermute | solution.py:46
  257.3 1.2 copy-start.2
  257.8 23.3 %copy-start.4 = (bf16[2048,256]{1,0:T(8,128)(2,1)S(1)}, bf16[2048,256]{1,0:T(8,128)(2,1)}, u32[]{:S(2)}) copy-start(bf16[2048,256]{1,0:T(8,128)(2,1)} %copy-done.3) | copy-start | bytes 3145732
  277.3 21.4 %collective-permute-start.6 = (bf16[2048,256]{1,0:T(8,128)(2,1)S(1)}, bf16[2048,256]{1,0:T(8,128)(2,1)S(1)}, u32[]{:S(2)}, u32[]{:S(2)}) collective-permute-start(bf16[2048,256]{1,0:T(8,128)(2,1)S(1)} %collective-permute-done.5), channel_id=1, source_target_pairs={{112,0},{0,16},{16,32},{32,48},{48,64},{64,80},{80,96},{96,112},{1... | collective-permute-start | bytes 3145736 | tf_op jit(solution)/shard_map/ppermute | solution.py:46
  283.3 15.5 %copy-start.7 = (s32[128]{0:T(128)S(1)}, s32[128]{0:T(128)}, u32[]{:S(2)}) copy-start(s32[128]{0:T(128)} %param.7) | copy-start | bytes 1540
  359.5 20.3 %copy-start.9 = (f32[2048,256]{1,0:T(8,128)S(1)}, f32[2048,256]{1,0:T(8,128)}, u32[]{:S(2)}) copy-start(f32[2048,256]{1,0:T(8,128)} %copy-done.8) | copy-start | bytes 6291460
  509.9 3.1 copy-start.5
Sparse Core Ops, SparseCore 0:
  13.4 54.3 all-gather.2
  390.8 119.0 all-reduce.2
where the time goes:
time: 522 us
  waiting for transfers between devices  285 us (55%)
  blocking collectives  152 us (29%)
  matrix products  42.2 us (8%)
  starting transfers between devices  16.4 us (3%)
  between operations  16.1 us (3%)
  local copies, waits for them, and re-layouts  6.82 us (1%)
    ppermute x7, waiting for transfers between devices, shifted(): return lax.ppermute(block, axis, route)  147 us
    psum x1, waiting for transfers between devices, shards(): first_grad, second_grad = lax.psum((first_grad, second_grad), BLK)  83 us
    all_gather x1, waiting for transfers between devices, shards(): pooled_all = lax.all_gather(pooled, GRP, axis=0, tiled=True)  54.5 us
    all_gather x1, blocking collectives, shards(): every_norm = lax.all_gather(log_norm, BLK_GRP, axis=0, tiled=True)  44.5 us
    all_to_all x2, blocking collectives, from_everyone(): lax.all_to_all(jnp.broadcast_to(array[None], (peers, *array.shape)), axis...  39.2 us
    psum x5, blocking collectives, by_axis(): array = lax.psum(array, axis)  35.6 us
    all_to_all x1, blocking collectives, sent_and_summed(): lax.all_to_all(in_blocks(array, dim, peers), axis, 0, 0, tiled=True)  32.5 us
    ppermute x7, starting transfers between devices, shifted(): return lax.ppermute(block, axis, route)  16.3 us
  transfers between devices with their start and end apart: 9, of which 9 were waited for; matrix products, arithmetic and copies ran while one was open for 1% of the time, Pallas kernels for 0%

commit v1 on v0

--- a/solution.py
+++ b/solution.py
@@ -67,7 +67,9 @@
     )
     summed = jnp.einsum("rf,rfc->rc", frame_mask, frames, preferred_element_type=jnp.float32)
     pooled = (summed / counts[:, None].astype(jnp.float32)).astype(jnp.bfloat16)
-    pooled_all = lax.all_gather(pooled, GRP, axis=0, tiled=True)
+    pooled_all = jnp.concatenate(
+        lax.all_to_all(jnp.stack([pooled] * lax.axis_size(GRP)), GRP, 0, 0), axis=0
+    )
     preact = jnp.dot(pooled_all, w_first, preferred_element_type=jnp.float32)
     hidden = jax.nn.gelu(preact).astype(jnp.bfloat16)
     raw_keys = sent_and_summed(

time: 522 us -> 568 us (1.088)
  blocking collectives: 152 us -> 251 us
  waiting for transfers between devices: 285 us -> 223 us
  starting transfers between devices: 16.4 us -> 24.4 us
    all_to_all x0 -> x1, blocking collectives: none -> 101 us  [shards(): lax.all_to_all(jnp.stack([pooled] * lax.axis_size(GRP)), GRP, 0, 0)]
    all_gather x1 -> x0, waiting for transfers between devices: 54.5 us -> none  [shards(): pooled_all = lax.all_gather(pooled, GRP, axis=0, tiled=True)]
    ppermute x7, starting transfers between devices: 16.3 us -> 24.4 us  [shifted(): return lax.ppermute(block, axis, route)]
    ppermute x7, waiting for transfers between devices: 147 us -> 140 us  [shifted(): return lax.ppermute(block, axis, route)]
  transfers between devices with their start and end apart: 9 -> 8, of which waited for: 9 -> 8; matrix products, arithmetic and copies ran while one was open for 1% -> 1% of each run, Pallas kernels for 0% -> 0%
where the time goes in v1:
time: 568 us; the launch traced here: 567 us
  blocking collectives  251 us (44%)
  waiting for transfers between devices  223 us (39%)
  matrix products  40.3 us (7%)
  starting transfers between devices  24.4 us (4%)
  between operations  16.1 us (3%)
  local copies, waits for them, and re-layouts  8.64 us (2%)
    ppermute x7, waiting for transfers between devices, shifted(): return lax.ppermute(block, axis, route)  140 us
    all_to_all x1, blocking collectives, shards(): lax.all_to_all(jnp.stack([pooled] * lax.axis_size(GRP)), GRP, 0, 0)  101 us
    psum x1, waiting for transfers between devices, shards(): first_grad, second_grad = lax.psum((first_grad, second_grad), BLK)  83 us
    all_gather x1, blocking collectives, shards(): every_norm = lax.all_gather(log_norm, BLK_GRP, axis=0, tiled=True)  45.6 us
    all_to_all x2, blocking collectives, from_everyone(): lax.all_to_all(jnp.broadcast_to(array[None], (peers, *array.shape)), axis...  39.1 us
    psum x5, blocking collectives, by_axis(): array = lax.psum(array, axis)  35.6 us
    all_to_all x1, blocking collectives, sent_and_summed(): lax.all_to_all(in_blocks(array, dim, peers), axis, 0, 0, tiled=True)  30.3 us
    ppermute x7, starting transfers between devices, shifted(): return lax.ppermute(block, axis, route)  24.4 us
  transfers between devices with their start and end apart: 8, of which 8 were waited for; matrix products, arithmetic and copies ran while one was open for 1% of the time, Pallas kernels for 0%

profile of v1, /device:TPU:6, one launch (start us, length us, event | category | flops | bytes accessed | tf_op | source)
XLA Modules:
  0.0 566.9 jit_solution(17816319701077877760)
XLA Ops:
  8.7 3.4 fusion.148
  13.6 100.8 %all_to_all.20 = bf16[16,128,2048]{2,1,0:T(8,128)(2,1)S(1)} all-to-all(bf16[16,128,2048]{2,1,0:T(8,128)(2,1)S(1)} %stack.2), channel_id=1, replica_groups=mesh['blk_0'=4,'blk_1'=2,'grp_0'=2,'grp_1'=4,'grp_2'=2] {'grp_0','grp_1'..., dimensions={0} | all-to-all | bytes 16777216 | tf_op jit(solution)/shard_map/all_to_all | solution.py:71
  118.9 30.3 %all_to_all.21 = f32[16,128,256]{2,1,0:T(8,128)S(1)} all-to-all(f32[16,128,256]{2,1,0:T(8,128)S(1)} %bitcast.58), channel_id=1, replica_groups=mesh['blk_0'=4,'blk_1'=2,'grp_0'=2,'grp_1'=4,'grp_2'=2] {'grp_0','grp_1'..., dimensions={0} | all-to-all | bytes 4194304 | tf_op jit(solution)/shard_map/all_to_all | solution.py:22
  149.7 19.1 %all_to_all.22 = bf16[16,128,256]{2,1,0:T(8,128)(2,1)S(1)} all-to-all(bf16[16,128,256]{2,1,0:T(8,128)(2,1)S(1)} %broadcast_in_dim.41), channel_id=1, replica_groups=mesh['blk_0'=4,'blk_1'=2,'grp_0'=2,'grp_1'=4,'grp_2'=2] {'grp_0','grp_1'..., dimensions={0} | all-to-all | bytes 2097152 | tf_op jit(solution)/shard_map/all_to_all | solution.py:34
  168.8 3.6 collective-permute-start
  172.4 23.0 %collective-permute-done = bf16[2048,256]{1,0:T(8,128)(2,1)S(1)} collective-permute-done((bf16[2048,256]{1,0:T(8,128)(2,1)S(1)}, bf16[2048,256]{1,0:T(8,128)(2,1)S(1)}, u32[]{:S(2)}, u32[]{:S(2)}) %collective-permute-start) | collective-permute-done | bytes 1048608 | tf_op jit(solution)/shard_map/ppermute | solution.py:46
  198.0 23.0 %collective-permute-done.1 = bf16[2048,256]{1,0:T(8,128)(2,1)S(1)} collective-permute-done((bf16[2048,256]{1,0:T(8,128)(2,1)S(1)}, bf16[2048,256]{1,0:T(8,128)(2,1)S(1)}, u32[]{:S(2)}, u32[]{:S(2)}) %collective-permute-start.1) | collective-permute-done | bytes 1048608 | tf_op jit(solution)/shard_map/ppermute | solution.py:46
  223.9 23.1 %collective-permute-done.2 = bf16[2048,256]{1,0:T(8,128)(2,1)S(1)} collective-permute-done((bf16[2048,256]{1,0:T(8,128)(2,1)S(1)}, bf16[2048,256]{1,0:T(8,128)(2,1)S(1)}, u32[]{:S(2)}, u32[]{:S(2)}) %collective-permute-start.2) | collective-permute-done | bytes 1048608 | tf_op jit(solution)/shard_map/ppermute | solution.py:46
  249.9 22.1 %collective-permute-done.3 = bf16[2048,256]{1,0:T(8,128)(2,1)} collective-permute-done((bf16[2048,256]{1,0:T(8,128)(2,1)S(1)}, bf16[2048,256]{1,0:T(8,128)(2,1)}, u32[]{:S(2)}, u32[]{:S(2)}) %collective-permute-start.3) | collective-permute-done | bytes 1048608 | tf_op jit(solution)/shard_map/ppermute | solution.py:46
  272.0 3.3 collective-permute-start.4
  275.4 20.1 %collective-permute-done.4 = bf16[2048,256]{1,0:T(8,128)(2,1)} collective-permute-done((bf16[2048,256]{1,0:T(8,128)(2,1)}, bf16[2048,256]{1,0:T(8,128)(2,1)}, u32[]{:S(2)}, u32[]{:S(2)}) %collective-permute-start.4) | collective-permute-done | bytes 1048608 | tf_op jit(solution)/shard_map/ppermute | solution.py:46
  295.5 4.9 collective-permute-start.5
  302.1 16.3 %collective-permute-done.5 = bf16[2048,256]{1,0:T(8,128)(2,1)S(1)} collective-permute-done((bf16[2048,256]{1,0:T(8,128)(2,1)}, bf16[2048,256]{1,0:T(8,128)(2,1)S(1)}, u32[]{:S(2)}, u32[]{:S(2)}) %collective-permute-start.5) | collective-permute-done | bytes 1048608 | tf_op jit(solution)/shard_map/ppermute | solution.py:46
  318.4 6.1 %collective-permute-start.6 = (bf16[2048,256]{1,0:T(8,128)(2,1)S(1)}, bf16[2048,256]{1,0:T(8,128)(2,1)S(1)}, u32[]{:S(2)}, u32[]{:S(2)}) collective-permute-start(bf16[2048,256]{1,0:T(8,128)(2,1)S(1)} %collective-permute-done.5), channel_id=1, source_target_pairs={{112,0},{0,16},{16,32},{32,48},{48,64},{64,80},{80,96},{96,112},{1... | collective-permute-start | bytes 3145736 | tf_op jit(solution)/shard_map/ppermute | solution.py:46
  328.9 12.4 %collective-permute-done.6 = bf16[2048,256]{1,0:T(8,128)(2,1)S(1)} collective-permute-done((bf16[2048,256]{1,0:T(8,128)(2,1)S(1)}, bf16[2048,256]{1,0:T(8,128)(2,1)S(1)}, u32[]{:S(2)}, u32[]{:S(2)}) %collective-permute-start.6) | collective-permute-done | bytes 1048608 | tf_op jit(solution)/shard_map/ppermute | solution.py:46
  345.2 45.6 %all-gather = f32[128,1,128]{2,1,0:T(1,128)S(1)} all-gather(f32[1,1,128]{2,1,0:T(1,128)S(1)} %bitcast.62), channel_id=1, replica_groups=mesh['blk_0'=4,'blk_1'=2,'grp_0'=2,'grp_1'=4,'grp_2'=2] {'blk_0','blk_1'..., dimensions={0}, use_global_device_ids=true | all-gather | bytes 66048 | tf_op jit(solution)/shard_map/all_gather | solution.py:111
  403.4 20.0 %all_to_all.23 = bf16[16,128,256]{2,1,0:T(8,128)(2,1)S(1)} all-to-all(bf16[16,128,256]{2,1,0:T(8,128)(2,1)S(1)} %broadcast_in_dim.42), channel_id=1, replica_groups=mesh['blk_0'=4,'blk_1'=2,'grp_0'=2,'grp_1'=4,'grp_2'=2] {'grp_0','grp_1'..., dimensions={0} | all-to-all | bytes 2097152 | tf_op jit(solution)/shard_map/all_to_all | solution.py:34
  423.4 9.3 %fusion.41 = f32[2048,256]{1,0:T(8,128)} fusion(bf16[2048,2048]{1,0:T(8,128)(2,1)} %bitcast.53, f32[2048,256]{1,0:T(8,128)} %copy-done.9, bf16[2048,256]{1,0:T(8,128)(2,1)S(1)} %bitcast.59, bf16[256,256]{1,0:T(8,128)(2,1)S(1)} %copy-done.7), kind=kOutput, calls=%fused_computation.114 | convolution fusion | flops 2426404864 | bytes 13762560 | tf_op jit(solution)/shard_map/dot_general | solution.py:145
  432.7 3.1 fusion.174
  435.8 8.9 %psum.49 = f32[]{:T(128)} all-reduce(f32[]{:T(128)} %get-tuple-element.35), channel_id=1, replica_groups=mesh['blk_0'=4,'blk_1'=2,'grp_0'=2,'grp_1'=4,'grp_2'=2] {'blk_0'}, use_global_device_ids=true, to_apply=%region_19.20 | all-reduce | flops 1 | bytes 8 | tf_op jit(solution)/shard_map/psum | solution.py:51
  444.7 7.3 %psum.50 = f32[]{:T(128)} all-reduce(f32[]{:T(128)} %psum.49), channel_id=1, replica_groups=mesh['blk_0'=4,'blk_1'=2,'grp_0'=2,'grp_1'=4,'grp_2'=2] {'blk_1'}, use_global_device_ids=true, to_apply=%region_20.21 | all-reduce | flops 1 | bytes 8 | tf_op jit(solution)/shard_map/psum | solution.py:51
  452.0 5.7 %psum.51 = f32[]{:T(128)} all-reduce(f32[]{:T(128)} %psum.50), channel_id=1, replica_groups=mesh['blk_0'=4,'blk_1'=2,'grp_0'=2,'grp_1'=4,'grp_2'=2] {'grp_0'}, use_global_device_ids=true, to_apply=%region_21.22 | all-reduce | flops 1 | bytes 8 | tf_op jit(solution)/shard_map/psum | solution.py:51
  457.7 10.6 %psum.52 = f32[]{:T(128)} all-reduce(f32[]{:T(128)} %psum.51), channel_id=1, replica_groups=mesh['blk_0'=4,'blk_1'=2,'grp_0'=2,'grp_1'=4,'grp_2'=2] {'grp_1'}, use_global_device_ids=true, to_apply=%region_22.23 | all-reduce | flops 1 | bytes 8 | tf_op jit(solution)/shard_map/psum | solution.py:51
  472.1 83.0 %all-reduce.3.cloned.1.call-done = (f32[2048,256]{1,0:T(8,128)}, f32[256,256]{1,0:T(8,128)}) async-done(((f32[2048,256]{1,0:T(8,128)}, f32[256,256]{1,0:T(8,128)}), (f32[2048,256]{1,0:T(8,128)}, f32[256,256]{1,0:T(8,128)})) %all-reduce.3.cloned.1.call-update) | async-done | bytes 2359312 | tf_op jit(solution)/shard_map/psum | solution.py:148
  (72 shorter events, 45.6 us)
Async XLA Ops:
  7.2 107.2 %copy-start = (bf16[2048,256]{1,0:T(8,128)(2,1)S(1)}, bf16[2048,256]{1,0:T(8,128)(2,1)}, u32[]{:S(2)}) copy-start(bf16[2048,256]{1,0:T(8,128)(2,1)} %param.8) | copy-start | bytes 3145732
  7.2 547.9 %all-reduce.3.cloned.1.call-start = ((), (), s32[]{:S(2)}) async-start(), calls=%async_computation.4 | async-start | bytes 4718592 | tf_op jit(solution)/shard_map/psum | solution.py:148
  114.4 3.2 copy-start.1
  114.4 3.2 copy-start.7
  117.6 1.3 copy-start.9
  168.8 26.6 %collective-permute-start = (bf16[2048,256]{1,0:T(8,128)(2,1)S(1)}, bf16[2048,256]{1,0:T(8,128)(2,1)S(1)}, u32[]{:S(2)}, u32[]{:S(2)}) collective-permute-start(bf16[2048,256]{1,0:T(8,128)(2,1)S(1)} %bitcast.54), channel_id=1, source_target_pairs={{112,0},{0,16},{16,32},{32,48},{48,64},{64,80},{80,96},{96,112},{1... | collective-permute-start | bytes 3145736 | tf_op jit(solution)/shard_map/ppermute | solution.py:46
  195.3 25.7 %collective-permute-start.1 = (bf16[2048,256]{1,0:T(8,128)(2,1)S(1)}, bf16[2048,256]{1,0:T(8,128)(2,1)S(1)}, u32[]{:S(2)}, u32[]{:S(2)}) collective-permute-start(bf16[2048,256]{1,0:T(8,128)(2,1)S(1)} %collective-permute-done), channel_id=1, source_target_pairs={{112,0},{0,16},{16,32},{32,48},{48,64},{64,80},{80,96},{96,112},{1... | collective-permute-start | bytes 3145736 | tf_op jit(solution)/shard_map/ppermute | solution.py:46
  221.0 1.1 copy-start.2
  222.1 24.8 %collective-permute-start.2 = (bf16[2048,256]{1,0:T(8,128)(2,1)S(1)}, bf16[2048,256]{1,0:T(8,128)(2,1)S(1)}, u32[]{:S(2)}, u32[]{:S(2)}) collective-permute-start(bf16[2048,256]{1,0:T(8,128)(2,1)S(1)} %collective-permute-done.1), channel_id=1, source_target_pairs={{112,0},{0,16},{16,32},{32,48},{48,64},{64,80},{80,96},{96,112},{1... | collective-permute-start | bytes 3145736 | tf_op jit(solution)/shard_map/ppermute | solution.py:46
  246.9 1.0 copy-start.4
  247.9 24.1 %collective-permute-start.3 = (bf16[2048,256]{1,0:T(8,128)(2,1)S(1)}, bf16[2048,256]{1,0:T(8,128)(2,1)}, u32[]{:S(2)}, u32[]{:S(2)}) collective-permute-start(bf16[2048,256]{1,0:T(8,128)(2,1)S(1)} %collective-permute-done.2), channel_id=1, source_target_pairs={{112,0},{0,16},{16,32},{32,48},{48,64},{64,80},{80,96},{96,112},{1... | collective-permute-start | bytes 3145736 | tf_op jit(solution)/shard_map/ppermute | solution.py:46
  272.0 23.4 %collective-permute-start.4 = (bf16[2048,256]{1,0:T(8,128)(2,1)}, bf16[2048,256]{1,0:T(8,128)(2,1)}, u32[]{:S(2)}, u32[]{:S(2)}) collective-permute-start(bf16[2048,256]{1,0:T(8,128)(2,1)} %collective-permute-done.3), channel_id=1, source_target_pairs={{112,0},{0,16},{16,32},{32,48},{48,64},{64,80},{80,96},{96,112},{1... | collective-permute-start | bytes 3145736 | tf_op jit(solution)/shard_map/ppermute | solution.py:46
  295.5 22.9 %collective-permute-start.5 = (bf16[2048,256]{1,0:T(8,128)(2,1)}, bf16[2048,256]{1,0:T(8,128)(2,1)S(1)}, u32[]{:S(2)}, u32[]{:S(2)}) collective-permute-start(bf16[2048,256]{1,0:T(8,128)(2,1)} %collective-permute-done.4), channel_id=1, source_target_pairs={{112,0},{0,16},{16,32},{32,48},{48,64},{64,80},{80,96},{96,112},{1... | collective-permute-start | bytes 3145736 | tf_op jit(solution)/shard_map/ppermute | solution.py:46
  300.4 1.2 copy-start.3
  300.9 23.6 %copy-start.5 = (bf16[2048,256]{1,0:T(8,128)(2,1)S(1)}, bf16[2048,256]{1,0:T(8,128)(2,1)}, u32[]{:S(2)}) copy-start(bf16[2048,256]{1,0:T(8,128)(2,1)} %copy-done.4) | copy-start | bytes 3145732
  318.4 22.9 %collective-permute-start.6 = (bf16[2048,256]{1,0:T(8,128)(2,1)S(1)}, bf16[2048,256]{1,0:T(8,128)(2,1)S(1)}, u32[]{:S(2)}, u32[]{:S(2)}) collective-permute-start(bf16[2048,256]{1,0:T(8,128)(2,1)S(1)} %collective-permute-done.5), channel_id=1, source_target_pairs={{112,0},{0,16},{16,32},{32,48},{48,64},{64,80},{80,96},{96,112},{1... | collective-permute-start | bytes 3145736 | tf_op jit(solution)/shard_map/ppermute | solution.py:46
  326.7 14.6 %copy-start.8 = (s32[128]{0:T(128)S(1)}, s32[128]{0:T(128)}, u32[]{:S(2)}) copy-start(s32[128]{0:T(128)} %param.7) | copy-start | bytes 1540
  555.1 3.1 copy-start.6
Sparse Core Ops, SparseCore 0:
  435.9 119.0 all-reduce.2
